TPU v7x, 32 devices: a whole 2x2x4 slice. The times are simulated.
32 devices in a mesh: curve: 16 (over z, y, core), tm: 2 (over x).
Axes of the slice: x: 2, y: 2, z: 4, core: 2. Of those that a mesh axis runs over, the one named last changes fastest.
Arguments:
- samples: float32 [4096, 65536], P('curve', 'tm'), may hold values from -30 to 30
- smoothing: float32 [4096], P('curve'), may hold values from 0.5 to 20
- test_matrix: float32 [4096, 64], P('tm'), may hold values from -0.75 to 0.75
- sketch_prev: float32 [4096, 64], P('tm', 'curve'), may hold values from -1.2 to 1.2
Outputs:
- coefficients: float32 [4096, 4096], P('curve', 'tm')
- scores: float32 [4096, 64], P('curve')
- sketch: float32 [4096, 64], P('tm', 'curve')
All inputs are finite; a program needn't handle non-finite values.
Results may differ from a plain program's by a relative error of at most 0.0002.
Values sent between devices are 32-bit elements; how exact they have to be, the bound alone decides.
No kernel may reach another device: no remote copies, remote signals or barrier semaphores. Data moves between devices by JAX's collectives and lax.ppermute only.
A program may use at most 192 MiB of HBM per device.

v0:
```python
import jax
import jax.numpy as jnp
from jax import lax
from jax.sharding import PartitionSpec as P

SPB = 16
ITERS = 4


damping = 0.45


def passed_along(block, axis, distance):
    devices = range(lax.axis_size(axis))
    route = [(i - distance, i) for i in devices if i - distance in devices]
    return lax.ppermute(block, axis, route)


def padded_2(block, sides, width):
    for axis, dim in sides:
        count = lax.axis_size(axis)
        forward = [(i, i + 1) for i in range(count - 1)]
        backward = [(target, source) for source, target in forward]
        low = lax.ppermute(
            lax.slice_in_dim(block, block.shape[dim] - width, None, axis=dim), axis, forward
        )
        high = lax.ppermute(lax.slice_in_dim(block, 0, width, axis=dim), axis, backward)
        block = jnp.concatenate([low, block, high], axis=dim)
    return block


def weight_table():
    frac = (jnp.arange(SPB, dtype=jnp.float32) + 0.5) / SPB
    pieces = [
        frac**3 / 6.0,
        (-3.0 * frac**3 + 3.0 * frac**2 + 3.0 * frac + 1.0) / 6.0,
        (3.0 * frac**3 - 6.0 * frac**2 + 4.0) / 6.0,
        (1.0 - frac) ** 3 / 6.0,
    ]
    return jnp.stack(pieces) / SPB


def relax_sweep(widened, target, smooth_col, index_wide, total_basis):
    second = widened[:, 2:] - 2.0 * widened[:, 1:-1] + widened[:, :-2]
    in_range = (index_wide[:-2] >= 0) & (index_wide[:-2] <= total_basis - 3)
    second = jnp.where(in_range[None, :], second, 0.0)
    bending = second[:, 2:] - 2.0 * second[:, 1:-1] + second[:, :-2]
    interior = widened[:, 2:-2]
    column_index = index_wide[2:-2]
    penalty_diag = (
        (column_index <= total_basis - 3).astype(jnp.float32)
        + 4.0 * ((column_index >= 1) & (column_index <= total_basis - 2)).astype(jnp.float32)
        + (column_index >= 2).astype(jnp.float32)
    )
    return interior + damping * (target - interior - smooth_col * bending) / (
        1.0 + smooth_col * penalty_diag
    )


def body(samples, smoothing, test_matrix, sketch_prev):
    row_count = samples.shape[0]
    basis_width = samples.shape[1] // SPB
    blocks = samples.reshape(row_count, basis_width, SPB)
    segment_sums = jnp.einsum(
        "cgq,mq->mcg", blocks, weight_table(), precision=lax.Precision.HIGHEST
    )
    padded = jnp.pad(segment_sums, ((0, 0), (0, 0), (3, 3)))
    extended = (
        padded[0, :, 0 : basis_width + 3]
        + padded[1, :, 1 : basis_width + 4]
        + padded[2, :, 2 : basis_width + 5]
        + padded[3, :, 3 : basis_width + 6]
    )
    spilled = extended[:, basis_width:]
    arrived = passed_along(spilled, "tm", 1)
    proj = jnp.concatenate([extended[:, :3] + arrived, extended[:, 3:basis_width]], axis=1)
    total_basis = basis_width * lax.axis_size("tm")
    first_column = lax.axis_index("tm") * basis_width
    smooth_col = smoothing[:, None]
    margin = 2 * ITERS
    proj_wide = padded_2(proj, (("tm", 1),), margin)
    coefficients = proj_wide
    for sweep_number in range(ITERS):
        margin_now = margin - 2 * sweep_number
        index_wide = (
            first_column - margin_now + jnp.arange(basis_width + 2 * margin_now, dtype=jnp.int32)
        )
        offset = 2 * sweep_number + 2
        target = proj_wide[:, offset : offset + basis_width + 2 * margin_now - 4]
        coefficients = relax_sweep(coefficients, target, smooth_col, index_wide, total_basis)
    curve_total = row_count * lax.axis_size("curve")
    totals = lax.psum(jnp.sum(coefficients, axis=0), "curve")
    column_mean = totals / curve_total
    centered = coefficients - column_mean[None, :]
    partial_value = jnp.dot(
        centered, test_matrix, precision=lax.Precision.HIGHEST, preferred_element_type=jnp.float32
    )
    scores = lax.psum(partial_value, "tm")
    sketch_part = (
        jnp.einsum("ck,cr->kr", centered, scores, precision=lax.Precision.HIGHEST) / curve_total
    )
    owned_part = lax.psum_scatter(sketch_part, "curve", scatter_dimension=1, tiled=True)
    return (coefficients, scores, sketch_prev + owned_part)


def solution(mesh):
    placed = (P("curve", "tm"), P("curve"), P("tm", None), P("tm", "curve"))
    return jax.shard_map(
        body,
        mesh=mesh,
        in_specs=placed,
        out_specs=(P("curve", "tm"), P("curve", None), P("tm", "curve")),
        check_vma=False,
    )
```

profile of v0, /device:TPU:0, one launch (start us, length us, event | category | flops | bytes accessed | tf_op | source)
XLA Modules:
  0.0 307.5 jit_solution(17813712295289506983)
XLA Ops:
  7.2 0.0 copy-start
  7.2 0.0 all-reduce.5.cloned.1.call-start
  7.3 33.5 %copy.12 = f32[256,32768]{0,1:T(8,128)} copy(f32[256,32768]{1,0:T(8,128)} %param.4) | data formatting | bytes 67108864 | tf_op args[0]
  40.7 35.7 %copy.13 = f32[256,2048,16]{1,2,0:T(8,128)} copy(f32[256,2048,16]{0,2,1:T(8,128)} %bitcast.9) | data formatting | bytes 67108864 | tf_op jit(solution)/shard_map/reshape | solution.py:63
  76.4 21.7 %fusion.43 = f32[4,256,2048]{2,0,1:T(4,128)S(1)} fusion(f32[256,2048,16]{1,2,0:T(8,128)} %copy.13, f32[1,16]{1,0:T(1,128)S(1)} %get-tuple-element.11, f32[1,16]{1,0:T(1,128)S(1)} %get-tuple-element.12, f32[1,16]{1,0:T(1,128)S(1)} %get-tuple-element.13, f32[1,16]{1,0:T(1,128)S(1)} %get-tuple-element.14), kind=kOutput, calls=%fused_computation.85 | convolution fusion | flops 402653440 | bytes 41943296 | tf_op jit(solution)/shard_map/cgq,mq->mcg/dot_general | solution.py:64
  98.1 16.1 %fusion.2 = f32[1,256,2051]{2,0,1:T(1,128)S(1)} fusion(f32[4,256,2048]{2,0,1:T(4,128)S(1)} %fusion.43), kind=kLoop, calls=%fused_computation.9 | loop fusion | flops 1575168 | bytes 10488832 | tf_op jit(solution)/shard_map/add | solution.py:69
  114.3 4.1 %copy.14 = f32[1,256,2051]{1,2,0:T(8,128)} copy(f32[1,256,2051]{2,0,1:T(1,128)S(1)} %fusion.2) | data formatting | bytes 4200448 | tf_op jit(solution)/shard_map/add | solution.py:69
  118.4 0.7 slice.196
  119.1 4.9 %collective-permute-start.1 = (f32[256,3]{0,1:T(4,128)S(1)}, f32[256,3]{0,1:T(4,128)S(1)}, u32[]{:S(2)}, u32[]{:S(2)}) collective-permute-start(f32[256,3]{0,1:T(4,128)S(1)} %slice.196), channel_id=1, source_target_pairs={{0,1},{2,3},{4,5},{6,7},{8,9},{10,11},{12,13},{14,15},{16,17},{18,... | collective-permute-start | bytes 9224 | tf_op jit(solution)/shard_map/ppermute | solution.py:16
  124.0 0.7 slice.194
  124.7 1.3 collective-permute-start
  126.0 0.1 convert_add_fusion.2
  126.1 0.1 convert_add_fusion.1
  126.2 0.1 convert_add_fusion
  126.3 0.1 convert_add_fusion.3
  126.3 1.7 slice.197
  128.1 0.0 copy-start.1
  128.1 0.0 collective-permute-done.1
  128.1 0.7 slice_add_fusion.8
  128.9 1.5 collective-permute-start.2
  130.3 0.0 collective-permute-done
  130.4 0.0 copy-done.1
  130.4 4.0 %collective-permute-done.2 = f32[256,8]{0,1:T(8,128)S(1)} collective-permute-done((f32[256,8]{0,1:T(8,128)S(1)}, f32[256,8]{0,1:T(8,128)S(1)}, u32[]{:S(2)}, u32[]{:S(2)}) %collective-permute-start.2) | collective-permute-done | bytes 8224 | tf_op jit(solution)/shard_map/ppermute | solution.py:27
  134.4 5.3 %concatenate.8 = f32[256,2064]{0,1:T(8,128)S(1)} concatenate(f32[256,8]{0,1:T(8,128)S(1)} %collective-permute-done, f32[256,3]{0,1:T(4,128)S(1)} %slice_add_fusion.8, f32[256,2045]{0,1:T(8,128)} %copy-done.1, f32[256,8]{0,1:T(8,128)S(1)} %collective-permute-done.2), dimensions={1} | concatenate | bytes 4227072 | tf_op jit(solution)/shard_map/concatenate | solution.py:28
  139.7 0.0 copy-start.5
  139.7 1.2 fusion.11
  140.9 1.7 fusion.9
  142.6 1.2 fusion.3
  143.8 1.8 fusion.27
  145.6 1.2 fusion.21
  146.8 1.8 fusion.19
  148.6 0.0 copy-start.2
  148.6 1.2 fusion.13
  149.8 0.4 copy-done.2
  150.2 1.8 fusion.56
  152.1 32.6 %psum.14 = f32[2048]{0:T(1024)S(1)} all-reduce(f32[2048]{0:T(1024)S(1)} %get-tuple-element.9), channel_id=1, replica_groups=mesh['curve'=16,'tm'=2] {'curve'}, use_global_device_ids=true, to_apply=%region_1.2 | all-reduce | flops 2048 | bytes 16384 | tf_op jit(solution)/shard_map/psum | solution.py:92
  184.6 2.1 fusion.37
  186.8 0.0 all-reduce.5.cloned.1.call-update
  186.8 0.0 all-reduce.7.cloned.1.call-start
  186.8 16.9 %all-reduce.5.cloned.1.call-done = f32[256,64]{0,1:T(8,128)} async-done(((f32[256,64]{0,1:T(8,128)}), f32[256,64]{0,1:T(8,128)}) %all-reduce.5.cloned.1.call-update) | async-done | bytes 65552 | tf_op jit(solution)/shard_map/psum | solution.py:98
  203.8 3.9 %convolution_multiply_fusion = f32[2048,64]{0,1:T(8,128)} fusion(f32[256,64]{0,1:T(8,128)} %all-reduce.5.cloned.1.call-done, f32[256,2048]{0,1:T(8,128)S(1)} %get-tuple-element.10, f32[2048]{0:T(1024)S(1)} %broadcast_multiply_fusion), kind=kOutput, calls=%fused_computation.6 | convolution fusion | flops 403308544 | bytes 2695168 | tf_op jit(solution)/shard_map/ck,cr->kr/dot_general | solution.py:100
  207.7 0.0 all-reduce.7.cloned.1.call-update
  207.7 0.0 copy-start.4
  207.7 0.6 dynamic-slice
  209.0 1.8 copy.15
  210.8 87.7 %all-reduce.7.cloned.1.call-done = f32[2048,64]{0,1:T(8,128)} async-done(((f32[2048,64]{0,1:T(8,128)}), f32[2048,64]{0,1:T(8,128)}) %all-reduce.7.cloned.1.call-update) | async-done | bytes 524304
  298.5 1.5 dynamic-slice_add_fusion
  300.0 0.6 copy.18
  (19 shorter events, 0.1 us)
Async XLA Ops:
  7.2 177.5 %copy-start = (f32[2048,64]{0,1:T(8,128)S(1)}, f32[2048,64]{0,1:T(8,128)}, u32[]{:S(2)}) copy-start(f32[2048,64]{0,1:T(8,128)} %param.6) | copy-start | bytes 1572868
  7.2 196.6 %all-reduce.5.cloned.1.call-start = ((), (), s32[]{:S(2)}) async-start(), calls=%async_computation | async-start | bytes 131072 | tf_op jit(solution)/shard_map/psum | solution.py:98
  119.1 9.0 %collective-permute-start.1 = (f32[256,3]{0,1:T(4,128)S(1)}, f32[256,3]{0,1:T(4,128)S(1)}, u32[]{:S(2)}, u32[]{:S(2)}) collective-permute-start(f32[256,3]{0,1:T(4,128)S(1)} %slice.196), channel_id=1, source_target_pairs={{0,1},{2,3},{4,5},{6,7},{8,9},{10,11},{12,13},{14,15},{16,17},{18,... | collective-permute-start | bytes 9224 | tf_op jit(solution)/shard_map/ppermute | solution.py:16
  124.7 5.7 %collective-permute-start = (f32[256,8]{0,1:T(8,128)S(1)}, f32[256,8]{0,1:T(8,128)S(1)}, u32[]{:S(2)}, u32[]{:S(2)}) collective-permute-start(f32[256,8]{0,1:T(8,128)S(1)} %slice.194), channel_id=1, source_target_pairs={{0,1},{2,3},{4,5},{6,7},{8,9},{10,11},{12,13},{14,15},{16,17},{18,... | collective-permute-start | bytes 24584 | tf_op jit(solution)/shard_map/ppermute | solution.py:24
  128.1 2.3 copy-start.1
  128.9 5.5 %collective-permute-start.2 = (f32[256,8]{0,1:T(8,128)S(1)}, f32[256,8]{0,1:T(8,128)S(1)}, u32[]{:S(2)}, u32[]{:S(2)}) collective-permute-start(f32[256,8]{0,1:T(8,128)S(1)} %fusion.41), channel_id=1, source_target_pairs={{1,0},{3,2},{5,4},{7,6},{9,8},{11,10},{13,12},{15,14},{17,16},{19,... | collective-permute-start | bytes 24584 | tf_op jit(solution)/shard_map/ppermute | solution.py:27
  139.7 1.2 copy-start.5
  148.6 1.6 copy-start.2
  186.8 21.0 %copy-start.6 = (u32[32]{0:T(128)S(1)}, u32[32]{0:T(128)}, u32[]{:S(2)}) copy-start(u32[32]{0:T(128)} %constant.48) | copy-start | bytes 388
  186.8 111.7 %all-reduce.7.cloned.1.call-start = ((), (), s32[]{:S(2)}) async-start(), calls=%async_computation.1 | async-start | bytes 1048576
  207.7 90.8 %copy-start.4 = (f32[2048,4]{0,1:T(4,128)S(1)}, f32[2048,4]{0,1:T(4,128)}, u32[]{:S(2)}) copy-start(f32[2048,4]{0,1:T(4,128)} %param.7) | copy-start | bytes 98308
  209.0 91.0 %copy-start.3 = (f32[256,64]{0,1:T(8,128)S(1)}, f32[256,64]{0,1:T(8,128)}, u32[]{:S(2)}) copy-start(f32[256,64]{0,1:T(8,128)} %all-reduce.5.cloned.1.call-done) | copy-start | bytes 196612
Sparse Core Ops, SparseCore 0:
  186.9 16.7 all-reduce.4
  207.8 90.6 all-reduce.6
where the time goes:
time: 309 us; the launch traced here: 307 us
  waiting for transfers between devices  109 us (35%)
  local copies, waits for them, and re-layouts  85.2 us (28%)
  blocking collectives  32.6 us (11%)
  other arithmetic  30.6 us (10%)
  matrix products  27.7 us (9%)
  between operations  15 us (5%)
  starting transfers between devices  7.68 us (2%)
    unnamed x3, waiting for transfers between devices  87.8 us
    unnamed x18, local copies, waits for them, and re-layouts  36.9 us
    reshape x1, local copies, waits for them, and re-layouts, body(): blocks = samples.reshape(row_count, basis_width, SPB)  35.7 us
    psum x1, blocking collectives, body(): totals = lax.psum(jnp.sum(coefficients, axis=0), 'curve')  32.6 us
    dot_general x1, matrix products, body(): jnp.einsum('cgq,mq->mcg', blocks, weight_table(), precision=lax.Precision...  21.7 us
    psum x1, waiting for transfers between devices, body(): scores = lax.psum(partial_value, 'tm')  16.9 us
    add x1, other arithmetic, body(): padded[0, :, 0:basis_width + 3] + padded[1, :, 1:basis_width + 4]  16.1 us
  transfers between devices with their start and end apart: 5, of which 3 were waited for; matrix products, arithmetic and copies ran while one was open for 2% of the time, Pallas kernels for 0%

commit v1 on v0

--- a/solution.py
+++ b/solution.py
@@ -1,13 +1,418 @@
+import functools
+
 import jax
 import jax.numpy as jnp
+import numpy as np
 from jax import lax
+from jax.experimental import pallas as pl
+from jax.experimental.pallas import tpu as pltpu
 from jax.sharding import PartitionSpec as P
 
 SPB = 16
 ITERS = 4
-
+LANES = 128
+TILE = LANES * SPB
+SPILL = TILE - 2 * LANES
+ZONE_LOW = 8
+ZONE_HIGH = 16
+EDGE = 24
 
 damping = 0.45
+
+
+def banded_weights():
+    frac = (np.arange(SPB, dtype=np.float64) + 0.5) / SPB
+    table = np.stack([
+        frac**3 / 6.0,
+        (-3.0 * frac**3 + 3.0 * frac**2 + 3.0 * frac + 1.0) / 6.0,
+        (3.0 * frac**3 - 6.0 * frac**2 + 4.0) / 6.0,
+        (1.0 - frac) ** 3 / 6.0,
+    ]) / SPB
+    weights = np.zeros((TILE, LANES), np.float32)
+    for segment in range(LANES):
+        for piece in range(4):
+            column = (segment + 3 - piece) % LANES
+            weights[segment * SPB : (segment + 1) * SPB, column] = table[piece]
+    high = weights.astype(jnp.bfloat16)
+    low = (weights - high.astype(np.float32)).astype(jnp.bfloat16)
+    return jnp.asarray(np.concatenate([high, low], axis=1))
+
+
+def split_bf16(value):
+    high = value.astype(jnp.bfloat16)
+    return high, (value - high.astype(jnp.float32)).astype(jnp.bfloat16)
+
+
+def dot32(a, b):
+    return jnp.dot(a, b, preferred_element_type=jnp.float32)
+
+
+def from_left(tiles, lane):
+    turned = [pltpu.roll(t, 1, 1) for t in tiles]
+    before = [jnp.zeros_like(turned[0])] + turned[:-1]
+    return [jnp.where(lane == 0, p, t) for p, t in zip(before, turned)]
+
+
+def from_right(tiles, lane):
+    turned = [pltpu.roll(t, LANES - 1, 1) for t in tiles]
+    after = turned[1:] + [jnp.zeros_like(turned[0])]
+    return [jnp.where(lane == LANES - 1, n, t) for n, t in zip(after, turned)]
+
+
+def second_difference(tiles, lane):
+    left, right = from_left(tiles, lane), from_right(tiles, lane)
+    return [(l + r) - (t + t) for l, t, r in zip(left, tiles, right)]
+
+
+def relax_rows(tiles, smooth, lane):
+    count = len(tiles)
+    diag_first = jnp.where(lane == 0, 1.0, jnp.where(lane == 1, 5.0, 6.0))
+    diag_last = jnp.where(lane == LANES - 1, 1.0, jnp.where(lane == LANES - 2, 5.0, 6.0))
+    factor = [damping / (1.0 + 6.0 * smooth)] * count
+    factor[0] = damping / (1.0 + smooth * diag_first)
+    factor[-1] = damping / (1.0 + smooth * diag_last)
+    if count == 1:
+        factor[0] = damping / (1.0 + smooth * jnp.minimum(diag_first, diag_last))
+    keep = {id(f): 1.0 - f for f in factor}
+    pull = {id(f): f * smooth for f in factor}
+    pulled = [f * t for f, t in zip(factor, tiles)]
+    state = tiles
+    for _ in range(ITERS):
+        second = second_difference(state, lane)
+        second[0] = jnp.where(lane == 0, 0.0, second[0])
+        second[-1] = jnp.where(lane == LANES - 1, 0.0, second[-1])
+        bending = second_difference(second, lane)
+        state = [
+            keep[id(f)] * t + p - pull[id(f)] * b
+            for f, t, p, b in zip(factor, state, pulled, bending)
+        ]
+    return state
+
+
+def curve_kernel(steps, step_rows, x_ref, smooth_ref, test_ref, w_ref, c_ref, msg_ref,
+                 lhs_ref, main_ref, last_ref, smooth_cols, test_cols, c_high, c_low, scored, edge_ref):
+    step = pl.program_id(0)
+    blocks = x_ref.shape[1] // TILE
+    rows = smooth_ref.shape[1]
+    rank = test_ref.shape[0]
+    has_left = lax.axis_index("tm") > 0
+    has_right = lax.axis_index("tm") < lax.axis_size("tm") - 1
+    lane = lax.broadcasted_iota(jnp.int32, (8, LANES), 1)
+
+    @pl.when(step == 0)
+    def _():
+        for at in range(0, rows, LANES):
+            part = jnp.broadcast_to(smooth_ref[:, at : at + LANES], (LANES, LANES))
+            smooth_cols[at : at + LANES, :] = part.T
+        for b in range(blocks):
+            part = test_ref[:, b * LANES : (b + 1) * LANES]
+            high, low = split_bf16(part)
+            both = jnp.concatenate([high.astype(jnp.float32), low.astype(jnp.float32)], axis=0)
+            test_cols[b * LANES : (b + 1) * LANES, :] = both.T.astype(jnp.bfloat16)
+
+    def relax_step():
+        slot = lax.rem(step + 1, 2)
+        first_row = pl.multiple_of(jnp.maximum(step - 1, 0) * step_rows, step_rows)
+        for group in range(0, step_rows, 16):
+            halves = []
+            for sub in (group, group + 8):
+                at = pl.ds(pl.multiple_of(first_row + sub, 8), 8)
+                smooth = smooth_cols[at, :]
+                last = [last_ref[slot, b * step_rows + sub : b * step_rows + sub + 8, :] for b in range(blocks)]
+                before = [jnp.zeros_like(last[0])] + last[:-1]
+                tiles = [
+                    main_ref[slot, b * step_rows + sub : b * step_rows + sub + 8, :]
+                    + jnp.where(lane < LANES // 2, before[b], last[b])
+                    for b in range(blocks)
+                ]
+                edge_right = jnp.where(
+                    lane < ZONE_HIGH,
+                    pltpu.roll(tiles[-1], ZONE_HIGH, 1),
+                    pltpu.roll(last[-1], ZONE_HIGH, 1),
+                )
+                edge_ref[at, :] = jnp.where(has_right, edge_right, tiles[0])
+                out = relax_rows(tiles, smooth, lane)
+                for b in range(blocks):
+                    c_ref[sub : sub + 8, b * LANES : (b + 1) * LANES] = out[b]
+                out[0] = jnp.where(jnp.logical_and(has_left, lane < ZONE_HIGH), 0.0, out[0])
+                out[-1] = jnp.where(
+                    jnp.logical_and(has_right, lane >= LANES - ZONE_LOW), 0.0, out[-1]
+                )
+                halves.append(out)
+            at = pl.ds(pl.multiple_of(first_row + group, 16), 16)
+            for b in range(blocks):
+                high, low = split_bf16(jnp.concatenate([halves[0][b], halves[1][b]], axis=0))
+                c_high[at, b * LANES : (b + 1) * LANES] = high
+                c_low[at, b * LANES : (b + 1) * LANES] = low
+
+    def project_step():
+        slot = lax.rem(step, 2)
+        for b in range(blocks):
+            high, low = split_bf16(x_ref[:, b * TILE : (b + 1) * TILE])
+            lhs_ref[b * step_rows : (b + 1) * step_rows, :TILE] = high
+            lhs_ref[b * step_rows : (b + 1) * step_rows, TILE:] = low
+        most = dot32(lhs_ref[:, :SPILL], w_ref[:SPILL, :]) + dot32(
+            lhs_ref[:, TILE : TILE + SPILL], w_ref[:SPILL, :]
+        )
+        main_ref[slot] = most[:, :LANES] + most[:, LANES:]
+        rest = dot32(lhs_ref[:, SPILL:TILE], w_ref[SPILL:, :]) + dot32(
+            lhs_ref[:, TILE + SPILL :], w_ref[SPILL:, :]
+        )
+        last_ref[slot] = rest[:, :LANES] + rest[:, LANES:]
+
+    @pl.when(step < steps)
+    def _():
+        relax_step()
+        project_step()
+
+    @pl.when(step == steps)
+    def _():
+        relax_step()
+        scored[...] = dot32(c_high[...], test_cols[...]) + dot32(c_low[...], test_cols[...])
+        for at in range(0, rows, LANES):
+            turned = scored[at : at + LANES, :].T
+            msg_ref[:rank, at : at + LANES] = turned[:rank] + turned[rank:]
+            msg_ref[rank : rank + EDGE, at : at + LANES] = edge_ref[at : at + LANES, :].T[:EDGE]
+        low_zone = padded_turn(test_ref[:, test_ref.shape[1] - LANES :])[LANES - ZONE_LOW :]
+        high_zone = padded_turn(test_ref[:, :LANES])
+        base = rank + EDGE
+        msg_ref[base:, :] = jnp.zeros_like(msg_ref[base:, :])
+        msg_ref[base:, :LANES] = jnp.where(has_right, low_zone, high_zone[:8])
+        msg_ref[base:, LANES : 2 * LANES] = high_zone[8:16]
+
+
+def padded_turn(part):
+    fill = jnp.zeros((LANES - part.shape[0], LANES), part.dtype)
+    return jnp.concatenate([part, fill], axis=0).T
+
+
+def curve_stage(samples, smooth_row, test_t, step_rows):
+    rows, width = samples.shape
+    rank, basis = test_t.shape
+    steps = rows // step_rows
+    stacked = step_rows * (width // TILE)
+    f32, bf16 = jnp.float32, jnp.bfloat16
+    return pl.pallas_call(
+        functools.partial(curve_kernel, steps, step_rows),
+        grid=(steps + 1,),
+        out_shape=(
+            jax.ShapeDtypeStruct((rows, basis), f32),
+            jax.ShapeDtypeStruct((rank + EDGE + 8, rows), f32),
+        ),
+        in_specs=[
+            pl.BlockSpec((step_rows, width), lambda i: (jnp.minimum(i, steps - 1), 0)),
+            pl.BlockSpec((1, rows), lambda i: (0, 0)),
+            pl.BlockSpec((rank, basis), lambda i: (0, 0)),
+            pl.BlockSpec((TILE, 2 * LANES), lambda i: (0, 0)),
+        ],
+        out_specs=(
+            pl.BlockSpec((step_rows, basis), lambda i: (jnp.maximum(i - 1, 0), 0)),
+            pl.BlockSpec((rank + EDGE + 8, rows), lambda i: (0, 0)),
+        ),
+        scratch_shapes=[
+            pltpu.VMEM((stacked, 2 * TILE), bf16),
+            pltpu.VMEM((2, stacked, LANES), f32),
+            pltpu.VMEM((2, stacked, LANES), f32),
+            pltpu.VMEM((rows, LANES), f32),
+            pltpu.VMEM((basis, 2 * rank), bf16),
+            pltpu.VMEM((rows, basis), bf16),
+            pltpu.VMEM((rows, basis), bf16),
+            pltpu.VMEM((rows, 2 * rank), f32),
+            pltpu.VMEM((rows, LANES), f32),
+        ],
+        compiler_params=pltpu.CompilerParams(
+            dimension_semantics=("arbitrary",), vmem_limit_bytes=40 * 1024 * 1024
+        ),
+        cost_estimate=pl.CostEstimate(
+            flops=4 * rows * width * 2 * LANES, bytes_accessed=4 * rows * width, transcendentals=0
+        ),
+        name="curves",
+    )(samples, smooth_row, test_t, banded_weights())
+
+
+def relax_strip(strip, smooth_row):
+    factor = damping / (1.0 + 6.0 * smooth_row)
+    pull = factor * smooth_row
+    height = strip.shape[0]
+    pulled = factor * strip
+    state = strip
+
+    def difference(v):
+        return pltpu.roll(v, 1, 0) + pltpu.roll(v, height - 1, 0) - (v + v)
+
+    for _ in range(ITERS):
+        state = (1.0 - factor) * state + pulled - pull * difference(difference(state))
+    return state
+
+
+def swapped(value, block, flip):
+    parts = [value[at : at + block] for at in range(0, value.shape[0], block)]
+    other = [parts[k ^ 1] for k in range(len(parts))]
+    return jnp.where(flip, jnp.concatenate(other, axis=0), value)
+
+
+def exchange_order(value, order, index):
+    count = 1 << len(order)
+    block = value.shape[0] // count
+    owner = [sum(b for k, b in enumerate(order) if p >> (len(order) - 1 - k) & 1) for p in range(count)]
+    value = jnp.concatenate([value[q * block : (q + 1) * block] for q in owner], axis=0)
+    for k, bit in enumerate(order):
+        value = swapped(value, value.shape[0] >> (k + 1), (index & bit) != 0)
+    return value
+
+
+def sketch_kernel(order, own_ref, came_ref, smooth_ref, c_in, c_ref, keep_ref, send_ref, total_ref,
+                  c_all, tile_ref, load_sem, store_sem):
+    rows, basis = c_in.shape
+    rank = total_ref.shape[0]
+    tiles = basis // LANES
+    half = rank // 2
+    has_left = lax.axis_index("tm") > 0
+    load = pltpu.make_async_copy(c_in, c_all, load_sem)
+    load.start()
+
+    own, came = own_ref[...], came_ref[...]
+    is_low = jnp.logical_not(has_left)
+    low = jnp.where(is_low, own, came)
+    high = jnp.where(is_low, came, own)
+    fill = jnp.zeros((EDGE - ZONE_LOW, rows), jnp.float32)
+    strip = jnp.concatenate([low[rank : rank + EDGE], fill], axis=0) + jnp.concatenate(
+        [fill, high[rank : rank + EDGE]], axis=0
+    )
+    fixed = relax_strip(strip, smooth_ref[...])[ZONE_LOW : ZONE_LOW + EDGE]
+    base = rank + EDGE
+    zone_test = jnp.concatenate(
+        [low[base:, :LANES], high[base:, :LANES], high[base:, LANES : 2 * LANES]], axis=0
+    )[:, :rank]
+    zone_scores = lax.dot_general(
+        zone_test, fixed, (((0,), (0,)), ((), ())),
+        precision=lax.Precision.HIGHEST, preferred_element_type=jnp.float32,
+    )
+    total = own[:rank] + came[:rank] + zone_scores
+    total_ref[...] = total
+
+    placed = jnp.where(
+        has_left,
+        jnp.concatenate([fixed[ZONE_LOW:], jnp.zeros((LANES - ZONE_HIGH, rows), jnp.float32)], axis=0),
+        jnp.concatenate([jnp.zeros((LANES - ZONE_LOW, rows), jnp.float32), fixed[:ZONE_LOW]], axis=0),
+    )
+    lane = lax.broadcasted_iota(jnp.int32, (LANES, LANES), 1)
+    first, past = jnp.where(has_left, 0, LANES - ZONE_LOW), jnp.where(has_left, ZONE_HIGH, LANES)
+    fix_lane = jnp.logical_and(lane >= first, lane < past)
+    edge = pl.multiple_of(jnp.where(has_left, 0, basis - LANES), LANES)
+
+    mean_score = jnp.mean(total, axis=1, keepdims=True)
+    spread = jnp.broadcast_to(mean_score, (rank, LANES))
+    score_row = padded_turn(spread)[:8]
+    index = lax.axis_index("curve")
+    spread = exchange_order(spread, order, index)
+    lhs_high, lhs_low = split_bf16(exchange_order(total - mean_score, order, index))
+    lhs = jnp.concatenate([lhs_high, lhs_low], axis=0)
+
+    load.wait()
+    for at in range(0, rows, LANES):
+        here = c_all[at : at + LANES, pl.ds(edge, LANES)]
+        here = jnp.where(fix_lane, placed[:, at : at + LANES].T, here)
+        tile_ref[at : at + LANES, :] = here
+        c_all[at : at + LANES, pl.ds(edge, LANES)] = here
+    store = pltpu.make_async_copy(tile_ref, c_ref.at[:, pl.ds(edge, LANES)], store_sem)
+    store.start()
+
+    for b in range(tiles):
+        block = c_all[:, b * LANES : (b + 1) * LANES]
+        mean = jnp.mean(block, axis=0, keepdims=True)
+        rhs_high, rhs_low = split_bf16(block - mean)
+        out = dot32(lhs, rhs_high)
+        out = out[:rank] + out[rank:] + dot32(lhs_high, rhs_low)
+        keep_ref[b * half : (b + 1) * half, :] = out[:half]
+        send_ref[b * half : (b + 1) * half, :] = out[half:]
+        at = (tiles + 1) * half + b
+        keep_ref[at : at + 1, :] = mean
+        send_ref[at : at + 1, :] = mean
+    at = tiles * half
+    keep_ref[at : at + half, :] = spread[:half]
+    send_ref[at : at + half, :] = spread[half:]
+    at = (tiles + 1) * half + tiles
+    keep_ref[at:, :] = score_row
+    send_ref[at:, :] = score_row
+    store.wait()
+
+
+def sketch_stage(own, came, smooth_row, coefficients, rank, order):
+    rows, basis = coefficients.shape
+    tiles = basis // LANES
+    half = rank // 2
+    f32 = jnp.float32
+    packed = jax.ShapeDtypeStruct(((tiles + 1) * half + tiles + 8, LANES), f32)
+    vmem, anywhere = pl.BlockSpec(memory_space=pltpu.VMEM), pl.BlockSpec(memory_space=pl.ANY)
+    return pl.pallas_call(
+        functools.partial(sketch_kernel, order),
+        out_shape=(
+            jax.ShapeDtypeStruct((rows, basis), f32), packed, packed,
+            jax.ShapeDtypeStruct((rank, rows), f32),
+        ),
+        in_specs=[vmem, vmem, vmem, anywhere],
+        out_specs=(anywhere, vmem, vmem, vmem),
+        scratch_shapes=[
+            pltpu.VMEM((rows, basis), f32),
+            pltpu.VMEM((rows, LANES), f32),
+            pltpu.SemaphoreType.DMA,
+            pltpu.SemaphoreType.DMA,
+        ],
+        input_output_aliases={3: 0},
+        compiler_params=pltpu.CompilerParams(vmem_limit_bytes=16 * 1024 * 1024),
+        cost_estimate=pl.CostEstimate(
+            flops=6 * rows * basis * rank, bytes_accessed=4 * rows * basis, transcendentals=0
+        ),
+        name="sketch_part",
+    )(own, came, smooth_row, coefficients)
+
+
+def unpack(packed, tiles, height):
+    moment = packed[: tiles * height].reshape(tiles, height, LANES)
+    score = packed[tiles * height : (tiles + 1) * height]
+    rest = packed[(tiles + 1) * height :]
+    return moment, score, rest
+
+
+def merged(keep, came, tiles, height, count):
+    moment, score, rest = unpack(keep, tiles, height)
+    moment_2, score_2, rest_2 = unpack(came, tiles, height)
+    apart = rest[:tiles] - rest_2[:tiles]
+    moment = moment + moment_2 + (0.5 * count) * apart[:, None, :] * (score - score_2)[None]
+    return moment, 0.5 * (score + score_2), 0.5 * (rest + rest_2)
+
+
+def packed_half(moment, score, rest, which):
+    height = moment.shape[1] // 2
+    part = slice(which * height, (which + 1) * height)
+    moment = moment[:, part].reshape(-1, LANES)
+    return jnp.concatenate([moment, score[part], rest], axis=0)
+
+
+def fast_body(samples, smoothing, test_matrix, sketch_prev):
+    rows, basis = samples.shape[0], test_matrix.shape[0]
+    rank = test_matrix.shape[1]
+    tiles = basis // LANES
+    groups = lax.axis_size("curve")
+    order = [1 << k for k in range(groups.bit_length() - 1)]
+    smooth_row = smoothing[None, :]
+    coefficients, message = curve_stage(samples, smooth_row, test_matrix.T, 32)
+    came = lax.ppermute(message, "tm", [(0, 1), (1, 0)])
+    coefficients, keep, send, total = sketch_stage(message, came, smooth_row, coefficients, rank, order)
+    height, count = rank // 2, rows
+    for bit in order:
+        came = lax.ppermute(send, "curve", [(i, i ^ bit) for i in range(groups)])
+        moment, score, rest = merged(keep, came, tiles, height, count)
+        count *= 2
+        if bit != order[-1]:
+            keep = packed_half(moment, score, rest, 0)
+            send = packed_half(moment, score, rest, 1)
+            height //= 2
+    score_mean = rest[tiles, :rank]
+    scores = (total - score_mean[:, None]).T
+    sketch = sketch_prev + moment.transpose(0, 2, 1).reshape(basis, height) / count
+    return coefficients, scores, sketch
 
 
 def passed_along(block, axis, distance):
@@ -57,7 +462,7 @@
     )
 
 
-def body(samples, smoothing, test_matrix, sketch_prev):
+def plain_body(samples, smoothing, test_matrix, sketch_prev):
     row_count = samples.shape[0]
     basis_width = samples.shape[1] // SPB
     blocks = samples.reshape(row_count, basis_width, SPB)
@@ -103,10 +508,15 @@
     return (coefficients, scores, sketch_prev + owned_part)
 
 
+def fits(mesh):
+    groups = mesh.shape["curve"]
+    return mesh.shape["tm"] == 2 and groups > 1 and groups & (groups - 1) == 0
+
+
 def solution(mesh):
     placed = (P("curve", "tm"), P("curve"), P("tm", None), P("tm", "curve"))
     return jax.shard_map(
-        body,
+        fast_body if fits(mesh) else plain_body,
         mesh=mesh,
         in_specs=placed,
         out_specs=(P("curve", "tm"), P("curve", None), P("tm", "curve")),

time: 309 us -> 55.3 us (0.18)
  waiting for transfers between devices: 109 us -> 13.4 us
  local copies, waits for them, and re-layouts: 85.2 us -> 3.01 us
  blocking collectives: 32.6 us -> 0 us
  other arithmetic: 30.6 us -> 1.54 us
  matrix products: 27.7 us -> 0 us
  Pallas kernels: 0 us -> 26.5 us
  between operations: 15 us -> 0.79 us
    unnamed x3 -> x0, waiting for transfers between devices: 87.8 us -> none
    reshape x1, local copies, waits for them, and re-layouts: 35.7 us -> 0.01 us  [packed_half(): moment = moment[:, part].reshape(-1, LANES)]
    unnamed x18 -> x8, local copies, waits for them, and re-layouts: 36.9 us -> 2.95 us
    psum x1 -> x0, blocking collectives: 32.6 us -> none  [body(): totals = lax.psum(jnp.sum(coefficients, axis=0), 'curve')]
    dot_general x3 -> x0, matrix products: 27.7 us -> none  [the longest x1 21.7 us: body(): jnp.einsum('cgq,mq->mcg', blocks, weight_table(), precision=lax.Precision...]
    pallas_call x0 -> x2, Pallas kernels: none -> 26.5 us  [the longest x1 24 us: curve_stage(): pl.pallas_call(functools.partial(curve_kernel, steps, step_rows), grid=(s...]
    add x14 -> x5, other arithmetic: 24 us -> 0.74 us  [the longest x1 0.64 us: fast_body(): sketch_prev + moment.transpose(0, 2, 1).reshape(basis, height) / count]
    psum x1 -> x0, waiting for transfers between devices: 16.9 us -> none  [body(): scores = lax.psum(partial_value, 'tm')]
  transfers between devices with their start and end apart: 5 -> 5, of which waited for: 3 -> 5; matrix products, arithmetic and copies ran while one was open for 2% -> 0% of each run, Pallas kernels for 0% -> 0%
where the time goes in v1:
time: 55.3 us; the launch traced here: 55 us
  Pallas kernels  26.5 us (48%)
  waiting for transfers between devices  13.4 us (24%)
  starting transfers between devices  9.69 us (18%)
  local copies, waits for them, and re-layouts  3.01 us (5%)
  other arithmetic  1.54 us (3%)
  between operations  0.79 us (1%)
    pallas_call x1, Pallas kernels, curve_stage(): pl.pallas_call(functools.partial(curve_kernel, steps, step_rows), grid=(s...  24 us
    ppermute x4, waiting for transfers between devices, fast_body(): came = lax.ppermute(send, 'curve', [(i, i ^ bit) for i in range(groups)])  10.6 us
    ppermute x4, starting transfers between devices, fast_body(): came = lax.ppermute(send, 'curve', [(i, i ^ bit) for i in range(groups)])  6.72 us
    ppermute x1, starting transfers between devices, fast_body(): came = lax.ppermute(message, 'tm', [(0, 1), (1, 0)])  2.97 us
    unnamed x8, local copies, waits for them, and re-layouts  2.95 us
    ppermute x1, waiting for transfers between devices, fast_body(): came = lax.ppermute(message, 'tm', [(0, 1), (1, 0)])  2.79 us
    pallas_call x1, Pallas kernels, sketch_stage(): pl.pallas_call(functools.partial(sketch_kernel, order), out_shape=(jax.Sh...  2.51 us
  transfers between devices with their start and end apart: 5, of which 5 were waited for; matrix products, arithmetic and copies ran while one was open for 0% of the time, Pallas kernels for 0%

profile of v1, /device:TPU:0, one launch (start us, length us, event | category | flops | bytes accessed | tf_op | source)
XLA Modules:
  0.0 55.0 jit_solution(6046908261455622219)
XLA Ops:
  0.6 0.0 copy-start
  0.6 1.2 %copy-done = bf16[2048,256]{1,0:T(8,128)(2,1)S(1)} copy-done((bf16[2048,256]{1,0:T(8,128)(2,1)S(1)}, bf16[2048,256]{1,0:T(8,128)(2,1)}, u32[]{:S(2)}) %copy-start) | copy-done | bytes 1048600
  1.9 0.0 copy-start.1
  1.9 1.0 %copy-done.1 = f32[2048,64]{0,1:T(8,128)S(1)} copy-done((f32[2048,64]{0,1:T(8,128)S(1)}, f32[2048,64]{0,1:T(8,128)}, u32[]{:S(2)}) %copy-start.1) | copy-done | bytes 524312
  2.9 0.0 copy-start.2
  2.9 0.7 %copy-done.2 = f32[256]{0:T(256)S(1)} copy-done((f32[256]{0:T(256)S(1)}, f32[256]{0:T(256)}, u32[]{:S(2)}) %copy-start.2) | copy-done | bytes 1048
  3.6 24.0 %curves.1 = (f32[256,2048]{1,0:T(8,128)}, f32[96,256]{1,0:T(8,128)S(1)}) custom-call(f32[256,32768]{1,0:T(8,128)} %x_ref.1, f32[1,256]{1,0:T(1,128)S(1)} %bitcast.26, f32[64,2048]{1,0:T(8,128)S(1)} %bitcast.25, bf16[2048,256]{1,0:T(8,128)(2,1)S(1)} %copy-done), custom_call_target="tpu_custom_call" | custom-call | flops 8589934592 | bytes 33554432 | tf_op jit(solution)/shard_map/curves/pallas_call | solution.py:195
  27.6 3.0 %collective-permute-start = (f32[96,256]{1,0:T(8,128)S(1)}, f32[96,256]{1,0:T(8,128)S(1)}, u32[]{:S(2)}, u32[]{:S(2)}) collective-permute-start(f32[96,256]{1,0:T(8,128)S(1)} %get-tuple-element.9.own_ref), channel_id=1, source_target_pairs={{0,1},{1,0},{2,3},{3,2},{4,5},{5,4},{6,7},{7,6},{8,9},{9,8},{10,11... | collective-permute-start | bytes 294920 | tf_op jit(solution)/shard_map/ppermute | solution.py:401
  30.6 2.8 %collective-permute-done.came_ref = f32[96,256]{1,0:T(8,128)S(1)} collective-permute-done((f32[96,256]{1,0:T(8,128)S(1)}, f32[96,256]{1,0:T(8,128)S(1)}, u32[]{:S(2)}, u32[]{:S(2)}) %collective-permute-start) | collective-permute-done | bytes 98336 | tf_op jit(solution)/shard_map/ppermute | solution.py:401
  33.4 2.5 %sketch_part.1 = (f32[256,2048]{1,0:T(8,128)}, f32[568,128]{1,0:T(8,128)S(1)}, f32[568,128]{1,0:T(8,128)S(1)}, f32[64,256]{1,0:T(8,128)S(1)}) custom-call(f32[96,256]{1,0:T(8,128)S(1)} %get-tuple-element.9.own_ref, f32[96,256]{1,0:T(8,128)S(1)} %collective-permute-done.came_ref, f32[1,256]{1,0:T(1,128)S(1)} %bitcast.27, ...), custom_call_target="tpu_custom_call", output_to_operand_aliasing={{0}: (3, {})} | custom-call | flops 201326592 | bytes 2097152 | tf_op jit(solution)/shard_map/sketch_part/pallas_call | solution.py:348
  35.9 0.0 copy-start.3
  35.9 0.1 collective-permute-start.1
  36.0 1.6 %collective-permute-done.1 = f32[568,128]{1,0:T(8,128)S(1)} collective-permute-done((f32[568,128]{1,0:T(8,128)S(1)}, f32[568,128]{1,0:T(8,128)S(1)}, u32[]{:S(2)}, u32[]{:S(2)}) %collective-permute-start.1) | collective-permute-done | bytes 290848 | tf_op jit(solution)/shard_map/ppermute | solution.py:405
  37.7 1.9 %collective-permute-start.2 = (f32[296,128]{1,0:T(8,128)S(1)}, f32[296,128]{1,0:T(8,128)S(1)}, u32[]{:S(2)}, u32[]{:S(2)}) collective-permute-start(f32[296,128]{1,0:T(8,128)S(1)} %pad_maximum_fusion), channel_id=1, source_target_pairs={{0,4},{2,6},{4,0},{6,2},{8,12},{10,14},{12,8},{14,10},{16,20},{18,... | collective-permute-start | bytes 454664 | tf_op jit(solution)/shard_map/ppermute | solution.py:405
  39.6 4.2 %collective-permute-done.2 = f32[296,128]{1,0:T(8,128)S(1)} collective-permute-done((f32[296,128]{1,0:T(8,128)S(1)}, f32[296,128]{1,0:T(8,128)S(1)}, u32[]{:S(2)}, u32[]{:S(2)}) %collective-permute-start.2) | collective-permute-done | bytes 151584 | tf_op jit(solution)/shard_map/ppermute | solution.py:405
  43.9 1.9 %collective-permute-start.3 = (f32[160,128]{1,0:T(8,128)S(1)}, f32[160,128]{1,0:T(8,128)S(1)}, u32[]{:S(2)}, u32[]{:S(2)}) collective-permute-start(f32[160,128]{1,0:T(8,128)S(1)} %pad_maximum_fusion.1), channel_id=1, source_target_pairs={{0,8},{2,10},{4,12},{6,14},{8,0},{10,2},{12,4},{14,6},{16,24},{18,... | collective-permute-start | bytes 245768 | tf_op jit(solution)/shard_map/ppermute | solution.py:405
  45.8 2.6 %collective-permute-done.3 = f32[160,128]{1,0:T(8,128)S(1)} collective-permute-done((f32[160,128]{1,0:T(8,128)S(1)}, f32[160,128]{1,0:T(8,128)S(1)}, u32[]{:S(2)}, u32[]{:S(2)}) %collective-permute-start.3) | collective-permute-done | bytes 81952 | tf_op jit(solution)/shard_map/ppermute | solution.py:405
  48.5 2.9 %collective-permute-start.4 = (f32[92,128]{1,0:T(8,128)S(1)}, f32[92,128]{1,0:T(8,128)S(1)}, u32[]{:S(2)}, u32[]{:S(2)}) collective-permute-start(f32[92,128]{1,0:T(8,128)S(1)} %pad_maximum_fusion.2), channel_id=1, source_target_pairs={{0,16},{2,18},{4,20},{6,22},{8,24},{10,26},{12,28},{14,30},{16,0},... | collective-permute-start | bytes 141320 | tf_op jit(solution)/shard_map/ppermute | solution.py:405
  51.4 2.2 %collective-permute-done.4 = f32[92,128]{1,0:T(8,128)S(1)} collective-permute-done((f32[92,128]{1,0:T(8,128)S(1)}, f32[92,128]{1,0:T(8,128)S(1)}, u32[]{:S(2)}, u32[]{:S(2)}) %collective-permute-start.4) | collective-permute-done | bytes 47136 | tf_op jit(solution)/shard_map/ppermute | solution.py:405
  53.6 0.7 %subtract_bitcast_fusion = f32[256,64]{0,1:T(8,128)} fusion(f32[64,256]{1,0:T(8,128)S(1)} %get-tuple-element.12, f32[64]{0:T(128)S(1)} %fusion.15), kind=kLoop, calls=%fused_computation.10 | loop fusion | flops 16384 | bytes 131328 | tf_op jit(solution)/shard_map/transpose | solution.py:413
  54.3 0.0 copy-done.3
  54.3 0.6 %fusion.6 = f32[2048,4]{0,1:T(4,128)} fusion(f32[2048,4]{0,1:T(4,128)S(1)} %copy-done.3, f32[16,4,128]{2,1,0:T(4,128)S(1)} %bitcast.32, f32[16,8,128]{2,1,0:T(8,128)S(1)} %fusion.2, f32[4,128]{1,0:T(4,128)S(1)} %slice_subtract_fusion.7, f32[16,128]{1,0:T(8,128)S(1)} %fusion.10), kind=kLoop, calls=%fused_computation.16 | loop fusion | flops 40960 | bytes 141312 | tf_op jit(solution)/shard_map/add | solution.py:414
  (27 shorter events, 0.3 us)
Async XLA Ops:
  0.6 1.2 %copy-start = (bf16[2048,256]{1,0:T(8,128)(2,1)S(1)}, bf16[2048,256]{1,0:T(8,128)(2,1)}, u32[]{:S(2)}) copy-start(bf16[2048,256]{1,0:T(8,128)(2,1)} %constant.5.clone.w_ref) | copy-start | bytes 3145732
  1.9 1.0 %copy-start.1 = (f32[2048,64]{0,1:T(8,128)S(1)}, f32[2048,64]{0,1:T(8,128)}, u32[]{:S(2)}) copy-start(f32[2048,64]{0,1:T(8,128)} %param.7) | copy-start | bytes 1572868
  2.9 0.7 %copy-start.2 = (f32[256]{0:T(256)S(1)}, f32[256]{0:T(256)}, u32[]{:S(2)}) copy-start(f32[256]{0:T(256)} %param.6) | copy-start | bytes 3076
  27.6 5.8 %collective-permute-start = (f32[96,256]{1,0:T(8,128)S(1)}, f32[96,256]{1,0:T(8,128)S(1)}, u32[]{:S(2)}, u32[]{:S(2)}) collective-permute-start(f32[96,256]{1,0:T(8,128)S(1)} %get-tuple-element.9.own_ref), channel_id=1, source_target_pairs={{0,1},{1,0},{2,3},{3,2},{4,5},{5,4},{6,7},{7,6},{8,9},{9,8},{10,11... | collective-permute-start | bytes 294920 | tf_op jit(solution)/shard_map/ppermute | solution.py:401
  35.9 18.4 %copy-start.3 = (f32[2048,4]{0,1:T(4,128)S(1)}, f32[2048,4]{0,1:T(4,128)}, u32[]{:S(2)}) copy-start(f32[2048,4]{0,1:T(4,128)} %param.8) | copy-start | bytes 98308
  35.9 1.6 %collective-permute-start.1 = (f32[568,128]{1,0:T(8,128)S(1)}, f32[568,128]{1,0:T(8,128)S(1)}, u32[]{:S(2)}, u32[]{:S(2)}) collective-permute-start(f32[568,128]{1,0:T(8,128)S(1)} %get-tuple-element.14), channel_id=1, source_target_pairs={{0,2},{2,0},{4,6},{6,4},{8,10},{10,8},{12,14},{14,12},{16,18},{18,... | collective-permute-start | bytes 872456 | tf_op jit(solution)/shard_map/ppermute | solution.py:405
  37.7 6.1 %collective-permute-start.2 = (f32[296,128]{1,0:T(8,128)S(1)}, f32[296,128]{1,0:T(8,128)S(1)}, u32[]{:S(2)}, u32[]{:S(2)}) collective-permute-start(f32[296,128]{1,0:T(8,128)S(1)} %pad_maximum_fusion), channel_id=1, source_target_pairs={{0,4},{2,6},{4,0},{6,2},{8,12},{10,14},{12,8},{14,10},{16,20},{18,... | collective-permute-start | bytes 454664 | tf_op jit(solution)/shard_map/ppermute | solution.py:405
  43.9 4.5 %collective-permute-start.3 = (f32[160,128]{1,0:T(8,128)S(1)}, f32[160,128]{1,0:T(8,128)S(1)}, u32[]{:S(2)}, u32[]{:S(2)}) collective-permute-start(f32[160,128]{1,0:T(8,128)S(1)} %pad_maximum_fusion.1), channel_id=1, source_target_pairs={{0,8},{2,10},{4,12},{6,14},{8,0},{10,2},{12,4},{14,6},{16,24},{18,... | collective-permute-start | bytes 245768 | tf_op jit(solution)/shard_map/ppermute | solution.py:405
  48.5 5.1 %collective-permute-start.4 = (f32[92,128]{1,0:T(8,128)S(1)}, f32[92,128]{1,0:T(8,128)S(1)}, u32[]{:S(2)}, u32[]{:S(2)}) collective-permute-start(f32[92,128]{1,0:T(8,128)S(1)} %pad_maximum_fusion.2), channel_id=1, source_target_pairs={{0,16},{2,18},{4,20},{6,22},{8,24},{10,26},{12,28},{14,30},{16,0},... | collective-permute-start | bytes 141320 | tf_op jit(solution)/shard_map/ppermute | solution.py:405
